TPU v7x, 256 devices: a whole 4x4x8 slice. The times are simulated.
256 devices in a mesh: section: 8 (over z_hi, core), expert: 32 (over z_lo, x, y).
Axes of the slice: x: 4, y: 4, z: 8 (z_hi: 4, z_lo: 2; z = z_hi * 2 + z_lo), core: 2. Of those that a mesh axis runs over, the one named last changes fastest.
Arguments:
- act_in: bfloat16 [8, 4096, 7168], P('section', 'expert'), may hold values from -6 to 6
- cotangent: bfloat16 [8, 4096, 7168], P('section', 'expert'), may hold values from -6 to 6
- fwd_ids: int32 [8, 4096, 8], P('section', 'expert'), may hold values from 0 to 255, as said below
- fwd_gates: float32 [8, 4096, 8], P('section', 'expert'), may hold values from 0.05 to 0.8
- bwd_ids: int32 [8, 4096, 8], P('section', 'expert'), may hold values from 0 to 255, as said below
- bwd_gates: float32 [8, 4096, 8], P('section', 'expert'), may hold values from 0.05 to 0.8
- gate_w: bfloat16 [8, 7168, 4096], P('section', None, 'expert'), may hold values from -0.0625 to 0.0625
- up_w: bfloat16 [8, 7168, 4096], P('section', None, 'expert'), may hold values from -0.0625 to 0.0625
- down_w: bfloat16 [8, 4096, 7168], P('section', 'expert'), may hold values from -0.125 to 0.125
- gate_pre: bfloat16 [8, 320, 4096], P('section', None, 'expert'), may hold values from -6 to 6
- up_pre: bfloat16 [8, 320, 4096], P('section', None, 'expert'), may hold values from -6 to 6
Outputs:
- next_act: bfloat16 [8, 4096, 7168], P('section', 'expert')
- prev_grad: bfloat16 [8, 4096, 7168], P('section', 'expert')
- gate_grad: float32 [8, 4096, 8], P('section', 'expert')
Inputs may be any that keep to these rules, and one draw needn't show every extreme that they name: `fwd_ids`: the 8 ids of a row differ. In each aligned block of 128 rows (the rows of one device) each id below 2 is named by at most 10 rows; in every section one such id is named by exactly 10 rows in every block. `bwd_ids`: as for fwd_ids.
All inputs are finite; a program needn't handle non-finite values.
Results may differ from a plain program's by a relative error of at most 0.012.
Values may be sent and summed in bfloat16 or wider, within the bound.
No kernel may reach another device: no remote copies, remote signals or barrier semaphores. Data moves between devices by JAX's collectives and lax.ppermute only.
A program may use at most 128 MiB of HBM per device.

v0:
```python
import math

import jax
import jax.numpy as jnp
from jax import lax
from jax.sharding import PartitionSpec as P

FF = 2048


def in_blocks(shard, dim, devices):
    before, after = (shard.shape[:dim], shard.shape[dim + 1 :])
    return jnp.moveaxis(shard.reshape(*before, devices, -1, *after), dim, 0)


def edges_of(length, count):
    turn = length // count
    if turn >= 8:
        turn -= turn % 8
    return [turn * k for k in range(1, count)]


def joined_along(pieces, dim):
    pieces = jnp.moveaxis(pieces, 0, dim)
    shape = pieces.shape
    return pieces.reshape(*shape[:dim], shape[dim] * shape[dim + 1], *shape[dim + 2 :])


def cut_exchange(shard, axis, pieces, split_dim, concat_dim):
    blocks = in_blocks(shard, split_dim, lax.axis_size(axis))
    cut = max(range(1, max(2, blocks.ndim - 1)), key=lambda d: blocks.shape[d])
    gathered = []
    for section in jnp.split(blocks, edges_of(blocks.shape[cut], pieces), axis=cut):
        if section.size:
            gathered.append(lax.all_to_all(section, axis, split_axis=0, concat_axis=0, tiled=True))
    return joined_along(jnp.concatenate(gathered, axis=cut), concat_dim)


def side_by_side(arrays, axis, split_dim, concat_dim, along):
    widths = [math.prod(a.shape[along:]) for a in arrays]
    both = jnp.concatenate(
        [a.reshape(*a.shape[:along], w) for a, w in zip(arrays, widths)], axis=along
    )
    result = lax.all_to_all(both, axis, split_axis=split_dim, concat_axis=concat_dim, tiled=True)
    pieces = jnp.split(result, [sum(widths[:k]) for k in range(1, len(widths))], axis=along)
    return tuple(
        (b.reshape(*result.shape[:along], *a.shape[along:]) for a, b in zip(arrays, pieces))
    )


def from_behind(value, axis, steps):
    count = lax.axis_size(axis)
    pairs = [(source, (source + steps) % count) for source in range(count)]
    return lax.ppermute(value, axis, pairs)


def routing(ids, gates, experts, capacity):
    expert_ids = jnp.arange(experts, dtype=jnp.int32)
    matches = ids[None, :, :] == expert_ids[:, None, None]
    routed = jnp.any(matches, axis=2)
    weights = jnp.sum(jnp.where(matches, gates[None, :, :], 0.0), axis=2)
    position = jnp.cumsum(routed.astype(jnp.int32), axis=1) - 1
    slot_ids = jnp.arange(capacity, dtype=jnp.int32)
    placing = (position[:, None, :] == slot_ids[None, :, None]) & routed[:, None, :]
    return (matches, placing.astype(jnp.float32), weights)


def send_rows(tokens, placing):
    buffer = jnp.einsum(
        "ect,td->ecd", placing.astype(jnp.bfloat16), tokens, preferred_element_type=jnp.float32
    ).astype(jnp.bfloat16)
    experts, capacity, width = buffer.shape
    ndev = lax.axis_size("expert")
    slices = ndev // experts
    received = lax.all_to_all(
        jnp.repeat(buffer, slices, axis=0), "expert", split_axis=0, concat_axis=0, tiled=True
    )
    return received.reshape(ndev * capacity, width)


def return_sums(partial_value, experts, capacity):
    ndev = lax.axis_size("expert")
    slices = ndev // experts
    width = partial_value.shape[1]
    rounded = partial_value.astype(jnp.bfloat16)
    back = cut_exchange(rounded.reshape(ndev, capacity, width), "expert", 2, 0, 0)
    return jnp.sum(back.reshape(experts, slices, capacity, width).astype(jnp.float32), axis=1)


def return_grads(partial_value, dots, experts, capacity):
    ndev = lax.axis_size("expert")
    slices = ndev // experts
    width = partial_value.shape[1]
    rounded = partial_value.astype(jnp.bfloat16)
    dots_rounded = dots.astype(jnp.bfloat16)
    back, back_dots = side_by_side(
        (rounded.reshape(ndev, capacity, width), dots_rounded.reshape(ndev, capacity)),
        "expert",
        0,
        0,
        2,
    )
    expert_grad = jnp.sum(
        back.reshape(experts, slices, capacity, width).astype(jnp.float32), axis=1
    )
    expert_dots = jnp.sum(back_dots.reshape(experts, slices, capacity).astype(jnp.float32), axis=1)
    return (expert_grad, expert_dots)


def body(
    act_in,
    cotangent,
    fwd_ids,
    fwd_gates,
    bwd_ids,
    bwd_gates,
    gate_w,
    up_w,
    down_w,
    gate_pre,
    up_pre,
):
    ndev = lax.axis_size("expert")
    w_gate = gate_w[0]
    w_up = up_w[0]
    w_down = down_w[0]
    ff_dev = w_gate.shape[1]
    slices = FF // ff_dev
    experts = ndev // slices
    capacity = gate_pre.shape[1] // ndev
    matches_f, placing_f, weights_f = routing(fwd_ids[0], fwd_gates[0], experts, capacity)
    slot_rows = send_rows(act_in[0], placing_f)
    gate_act = jnp.dot(slot_rows, w_gate, preferred_element_type=jnp.float32)
    up_act = jnp.dot(slot_rows, w_up, preferred_element_type=jnp.float32)
    hidden = (jax.nn.silu(gate_act) * up_act).astype(jnp.bfloat16)
    expert_out = return_sums(
        jnp.dot(hidden, w_down, preferred_element_type=jnp.float32), experts, capacity
    )
    mixed = jnp.einsum(
        "ect,ecd->td",
        placing_f * weights_f[:, None, :],
        expert_out,
        precision=lax.Precision.HIGHEST,
    )
    matches_b, placing_b, weights_b = routing(bwd_ids[0], bwd_gates[0], experts, capacity)
    grad_rows = send_rows(cotangent[0], placing_b)
    saved_gate = gate_pre[0].astype(jnp.float32)
    saved_up = up_pre[0].astype(jnp.float32)
    grad_hidden = jnp.einsum("rd,fd->rf", grad_rows, w_down, preferred_element_type=jnp.float32)
    sigmoid_gate = jax.nn.sigmoid(saved_gate)
    activated = saved_gate * sigmoid_gate
    gate_dots = jnp.sum(grad_hidden * activated * saved_up, axis=1)
    grad_gate_act = (
        grad_hidden * saved_up * sigmoid_gate * (1.0 + saved_gate * (1.0 - sigmoid_gate))
    ).astype(jnp.bfloat16)
    grad_up_act = (grad_hidden * activated).astype(jnp.bfloat16)
    grad_partial = jnp.einsum(
        "rf,df->rd", grad_gate_act, w_gate, preferred_element_type=jnp.float32
    )
    grad_partial = grad_partial + jnp.einsum(
        "rf,df->rd", grad_up_act, w_up, preferred_element_type=jnp.float32
    )
    expert_grad, expert_dots = return_grads(grad_partial, gate_dots, experts, capacity)
    input_grad = jnp.einsum(
        "ect,ecd->td",
        placing_b * weights_b[:, None, :],
        expert_grad,
        precision=lax.Precision.HIGHEST,
    )
    token_dots = jnp.einsum("ect,ec->et", placing_b, expert_dots, precision=lax.Precision.HIGHEST)
    gate_grad = jnp.sum(jnp.where(matches_b, token_dots[:, :, None], 0.0), axis=0)
    next_act = from_behind(mixed.astype(jnp.bfloat16)[None], "section", 1)
    prev_grad = from_behind(input_grad.astype(jnp.bfloat16)[None], "section", -1)
    return (next_act, prev_grad, gate_grad[None])


def solution(mesh):
    in_specs = (
        P("section", "expert", None),
        P("section", "expert", None),
        P("section", "expert", None),
        P("section", "expert", None),
        P("section", "expert", None),
        P("section", "expert", None),
        P("section", None, "expert"),
        P("section", None, "expert"),
        P("section", "expert", None),
        P("section", None, "expert"),
        P("section", None, "expert"),
    )
    out_specs = (
        P("section", "expert", None),
        P("section", "expert", None),
        P("section", "expert", None),
    )
    return jax.shard_map(body, mesh=mesh, in_specs=in_specs, out_specs=out_specs, check_vma=False)
```

profile of v0, /device:TPU:1, one launch (start us, length us, event | category | flops | bytes accessed | tf_op | source)
XLA Modules:
  0.0 520.6 jit_solution(15371524996227572271)
XLA Ops:
  3.7 3.9 broadcast_in_dim.61
  7.5 9.5 %all-to-all-start = ((bf16[32,10,7168]{2,1,0:T(8,128)(2,1)}), bf16[32,10,7168]{2,1,0:T(8,128)(2,1)}, u32[]{:S(2)}, u32[]{:S(2)}) async-start(bf16[32,10,7168]{2,1,0:T(8,128)(2,1)} %bitcast.95), calls=%async_computation | async-start | bytes 14680064 | tf_op jit(solution)/shard_map/all_to_all | solution.py:75
  17.4 1.9 convolution_convert_fusion.1
  19.2 101.9 %all-to-all-done = bf16[32,10,7168]{2,1,0:T(8,128)(2,1)} async-done(((bf16[32,10,7168]{2,1,0:T(8,128)(2,1)}), bf16[32,10,7168]{2,1,0:T(8,128)(2,1)}, u32[]{:S(2)}, u32[]{:S(2)}) %all-to-all-start) | async-done | bytes 4587552 | tf_op jit(solution)/shard_map/all_to_all | solution.py:75
  121.1 3.9 broadcast_in_dim.65
  125.0 7.4 %all-to-all-start.3 = ((bf16[32,10,7168]{2,1,0:T(8,128)(2,1)}), bf16[32,10,7168]{2,1,0:T(8,128)(2,1)}, u32[]{:S(2)}, u32[]{:S(2)}) async-start(bf16[32,10,7168]{2,1,0:T(8,128)(2,1)} %bitcast.94), calls=%async_computation.3 | async-start | bytes 14680064 | tf_op jit(solution)/shard_map/all_to_all | solution.py:75
  132.4 8.0 %reshape.67 = bf16[320,7168]{1,0:T(8,128)(2,1)} reshape(bf16[32,10,7168]{2,1,0:T(8,128)(2,1)} %all-to-all-done) | data formatting | bytes 9175040 | tf_op jit(solution)/shard_map/reshape | solution.py:78
  140.5 4.2 fusion.14
  144.7 10.0 %convolution_convert_fusion = bf16[320,7168]{1,0:T(8,128)(2,1)} fusion(bf16[1,128,7168]{2,1,0:T(8,128)(2,1)} %param.19, bf16[320,7168]{1,0:T(8,128)(2,1)} %reshape.67, bf16[1,7168,128]{2,1,0:T(8,128)(2,1)S(1)} %copy-done, f32[320,128]{1,0:T(8,128)S(1)} %fusion.14), kind=kOutput, calls=%fused_computation.3 | convolution fusion | flops 1176944640 | bytes 13008896 | tf_op jit(solution)/shard_map/dot_general | solution.py:137
  154.7 7.8 %reshape_reshape.2 = bf16[32,1,10,7168]{3,2,0,1:T(8,128)(2,1)} reshape(bf16[320,7168]{1,0:T(8,128)(2,1)} %convolution_convert_fusion) | data formatting | bytes 9175040 | tf_op jit(solution)/shard_map/reshape;reshape | solution.py:13
  162.5 6.7 %slice_bitcast_fusion.1 = (bf16[32,1,5,7168]{3,2,1,0:T(8,128)(2,1)}, bf16[32,1,5,7168]{3,2,1,0:T(8,128)(2,1)}) fusion(bf16[32,1,10,7168]{3,2,0,1:T(8,128)(2,1)} %reshape_reshape.2), kind=kLoop, calls=%fused_computation.16 | loop fusion | bytes 9175040 | tf_op jit(solution)/shard_map/split | solution.py:33
  169.2 55.6 %all-to-all-done.3 = bf16[32,10,7168]{2,1,0:T(8,128)(2,1)} async-done(((bf16[32,10,7168]{2,1,0:T(8,128)(2,1)}), bf16[32,10,7168]{2,1,0:T(8,128)(2,1)}, u32[]{:S(2)}, u32[]{:S(2)}) %all-to-all-start.3) | async-done | bytes 4587552 | tf_op jit(solution)/shard_map/all_to_all | solution.py:75
  224.8 55.1 %all_to_all.25 = bf16[32,1,5,7168]{3,2,1,0:T(8,128)(2,1)} all-to-all(bf16[32,1,5,7168]{3,2,1,0:T(8,128)(2,1)} %get-tuple-element.5), channel_id=1, replica_groups=mesh['section'=8,'expert'=32] {'expert'}, dimensions={0} | all-to-all | bytes 4587520 | tf_op jit(solution)/shard_map/all_to_all | solution.py:35
  279.9 5.9 %all-to-all-start.2 = ((bf16[32,1,5,7168]{3,2,1,0:T(8,128)(2,1)}), bf16[32,1,5,7168]{3,2,1,0:T(8,128)(2,1)}, u32[]{:S(2)}, u32[]{:S(2)}) async-start(bf16[32,1,5,7168]{3,2,1,0:T(8,128)(2,1)} %get-tuple-element.6), calls=%async_computation.2 | async-start | bytes 7340032 | tf_op jit(solution)/shard_map/all_to_all | solution.py:35
  285.8 8.1 %reshape.69 = bf16[320,7168]{1,0:T(8,128)(2,1)} reshape(bf16[32,10,7168]{2,1,0:T(8,128)(2,1)} %all-to-all-done.3) | data formatting | bytes 9175040 | tf_op jit(solution)/shard_map/reshape | solution.py:78
  294.0 4.5 fusion.29
  299.8 3.4 fusion
  303.2 7.8 %reshape.70 = bf16[32,10,7168]{2,1,0:T(8,128)(2,1)} reshape(bf16[320,7168]{1,0:T(8,128)(2,1)} %fusion) | data formatting | bytes 9175040 | tf_op jit(solution)/shard_map/reshape | solution.py:97
  311.3 6.8 %pad_maximum_fusion = bf16[32,10,7169]{2,1,0:T(8,128)(2,1)} fusion(bf16[32,10,1]{2,1,0:T(8,128)(2,1)S(1)} %convert_element_type.136, bf16[32,10,7168]{2,1,0:T(8,128)(2,1)} %reshape.70), kind=kLoop, calls=%fused_computation.13 | loop fusion | flops 9176320 | bytes 9176320 | tf_op jit(solution)/shard_map/concatenate | solution.py:41
  318.1 12.1 %all-to-all-done.2 = bf16[32,1,5,7168]{3,2,1,0:T(8,128)(2,1)} async-done(((bf16[32,1,5,7168]{3,2,1,0:T(8,128)(2,1)}), bf16[32,1,5,7168]{3,2,1,0:T(8,128)(2,1)}, u32[]{:S(2)}, u32[]{:S(2)}) %all-to-all-start.2) | async-done | bytes 2293792 | tf_op jit(solution)/shard_map/all_to_all | solution.py:35
  330.2 8.8 %all-to-all-start.4 = ((bf16[32,10,7169]{2,1,0:T(8,128)(2,1)}), bf16[32,10,7169]{2,1,0:T(8,128)(2,1)}, u32[]{:S(2)}, u32[]{:S(2)}) async-start(bf16[32,10,7169]{2,1,0:T(8,128)(2,1)} %pad_maximum_fusion), calls=%async_computation.4 | async-start | bytes 14942208 | tf_op jit(solution)/shard_map/all_to_all | solution.py:44
  339.1 5.6 %pad_maximum_fusion.1 = bf16[32,1,10,7168]{3,2,1,0:T(8,128)(2,1)S(1)} fusion(bf16[32,1,5,7168]{3,2,1,0:T(8,128)(2,1)} %all-to-all-done.2, bf16[32,1,5,7168]{3,2,1,0:T(8,128)(2,1)} %all_to_all.25), kind=kLoop, calls=%fused_computation.14 | loop fusion | flops 9175040 | bytes 9175040 | tf_op jit(solution)/shard_map/concatenate | solution.py:36
  346.1 4.2 fusion.4
  350.3 4.5 collective-permute-start
  354.9 102.7 %all-to-all-done.4 = bf16[32,10,7169]{2,1,0:T(8,128)(2,1)} async-done(((bf16[32,10,7169]{2,1,0:T(8,128)(2,1)}), bf16[32,10,7169]{2,1,0:T(8,128)(2,1)}, u32[]{:S(2)}, u32[]{:S(2)}) %all-to-all-start.4) | async-done | bytes 4588192 | tf_op jit(solution)/shard_map/all_to_all | solution.py:44
  459.1 3.8 split.18
  463.0 4.2 convert_reduce_fusion.1
  467.7 3.1 fusion.3
  470.8 3.9 collective-permute-start.1
  474.8 4.2 collective-permute-done
  479.0 37.5 %collective-permute-done.1 = bf16[1,128,7168]{2,1,0:T(8,128)(2,1)S(1)} collective-permute-done((bf16[1,128,7168]{2,1,0:T(8,128)(2,1)S(1)}, bf16[1,128,7168]{2,1,0:T(8,128)(2,1)S(1)}, u32[]{:S(2)}, u32[]{:S(2)}) %collective-permute-start.1) | collective-permute-done | bytes 1835040 | tf_op jit(solution)/shard_map/ppermute | solution.py:54
  516.5 2.8 copy.68
  (38 shorter events, 9.7 us)
Async XLA Ops:
  0.6 144.1 %copy-start = (bf16[1,7168,128]{2,1,0:T(8,128)(2,1)S(1)}, bf16[1,7168,128]{2,1,0:T(8,128)(2,1)}, u32[]{:S(2)}) copy-start(bf16[1,7168,128]{2,1,0:T(8,128)(2,1)} %param.18) | copy-start | bytes 5505028
  7.5 9.5 %copy-start.4 = (s32[1,128,8]{1,2,0:T(8,128)S(1)}, s32[1,128,8]{1,2,0:T(8,128)}, u32[]{:S(2)}) copy-start(s32[1,128,8]{1,2,0:T(8,128)} %param.15) | copy-start | bytes 12292
  7.5 113.6 %all-to-all-start = ((bf16[32,10,7168]{2,1,0:T(8,128)(2,1)}), bf16[32,10,7168]{2,1,0:T(8,128)(2,1)}, u32[]{:S(2)}, u32[]{:S(2)}) async-start(bf16[32,10,7168]{2,1,0:T(8,128)(2,1)} %bitcast.95), calls=%async_computation | async-start | bytes 14680064 | tf_op jit(solution)/shard_map/all_to_all | solution.py:75
  125.0 99.8 %all-to-all-start.3 = ((bf16[32,10,7168]{2,1,0:T(8,128)(2,1)}), bf16[32,10,7168]{2,1,0:T(8,128)(2,1)}, u32[]{:S(2)}, u32[]{:S(2)}) async-start(bf16[32,10,7168]{2,1,0:T(8,128)(2,1)} %bitcast.94), calls=%async_computation.3 | async-start | bytes 14680064 | tf_op jit(solution)/shard_map/all_to_all | solution.py:75
  279.9 50.3 %all-to-all-start.2 = ((bf16[32,1,5,7168]{3,2,1,0:T(8,128)(2,1)}), bf16[32,1,5,7168]{3,2,1,0:T(8,128)(2,1)}, u32[]{:S(2)}, u32[]{:S(2)}) async-start(bf16[32,1,5,7168]{3,2,1,0:T(8,128)(2,1)} %get-tuple-element.6), calls=%async_computation.2 | async-start | bytes 7340032 | tf_op jit(solution)/shard_map/all_to_all | solution.py:35
  285.8 8.2 %copy-start.2 = (bf16[1,320,128]{2,1,0:T(8,128)(2,1)S(1)}, bf16[1,320,128]{2,1,0:T(8,128)(2,1)}, u32[]{:S(2)}) copy-start(bf16[1,320,128]{2,1,0:T(8,128)(2,1)} %param.20) | copy-start | bytes 245764
  285.8 8.2 %copy-start.3 = (bf16[1,320,128]{2,1,0:T(8,128)(2,1)S(1)}, bf16[1,320,128]{2,1,0:T(8,128)(2,1)}, u32[]{:S(2)}) copy-start(bf16[1,320,128]{2,1,0:T(8,128)(2,1)} %param.21) | copy-start | bytes 245764
  294.0 4.5 copy-start.1
  318.1 21.0 %copy-start.5 = (s32[1,128,8]{1,2,0:T(8,128)S(1)}, s32[1,128,8]{1,2,0:T(8,128)}, u32[]{:S(2)}) copy-start(s32[1,128,8]{1,2,0:T(8,128)} %param.13) | copy-start | bytes 12292
  318.1 21.0 %copy-start.7 = (f32[1,128,8]{1,2,0:T(8,128)S(1)}, f32[1,128,8]{1,2,0:T(8,128)}, u32[]{:S(2)}) copy-start(f32[1,128,8]{1,2,0:T(8,128)} %param.14) | copy-start | bytes 12292
  330.2 127.4 %all-to-all-start.4 = ((bf16[32,10,7169]{2,1,0:T(8,128)(2,1)}), bf16[32,10,7169]{2,1,0:T(8,128)(2,1)}, u32[]{:S(2)}, u32[]{:S(2)}) async-start(bf16[32,10,7169]{2,1,0:T(8,128)(2,1)} %pad_maximum_fusion), calls=%async_computation.4 | async-start | bytes 14942208 | tf_op jit(solution)/shard_map/all_to_all | solution.py:44
  350.3 128.6 %collective-permute-start = (bf16[1,128,7168]{2,1,0:T(8,128)(2,1)}, bf16[1,128,7168]{2,1,0:T(8,128)(2,1)}, u32[]{:S(2)}, u32[]{:S(2)}) collective-permute-start(bf16[1,128,7168]{2,1,0:T(8,128)(2,1)} %fusion.4), channel_id=1, source_target_pairs={{0,32},{32,64},{64,96},{96,128},{128,160},{160,192},{192,224},{224... | collective-permute-start | bytes 5505032 | tf_op jit(solution)/shard_map/ppermute | solution.py:54
  462.9 4.2 copy-start.6
  470.8 45.7 %collective-permute-start.1 = (bf16[1,128,7168]{2,1,0:T(8,128)(2,1)S(1)}, bf16[1,128,7168]{2,1,0:T(8,128)(2,1)S(1)}, u32[]{:S(2)}, u32[]{:S(2)}) collective-permute-start(bf16[1,128,7168]{2,1,0:T(8,128)(2,1)S(1)} %fusion.3), channel_id=1, source_target_pairs={{0,224},{32,0},{64,32},{96,64},{128,96},{160,128},{192,160},{224,1... | collective-permute-start | bytes 5505032 | tf_op jit(solution)/shard_map/ppermute | solution.py:54
where the time goes:
time: 528 us; the launch traced here: 521 us
  waiting for transfers between devices  314 us (59%)
  local copies, waits for them, and re-layouts  55.7 us (11%)
  blocking collectives  55.1 us (10%)
  starting transfers between devices  40 us (8%)
  matrix products  34.7 us (7%)
  other arithmetic  20.2 us (4%)
    all_to_all x2, waiting for transfers between devices, send_rows(): lax.all_to_all(jnp.repeat(buffer, slices, axis=0), 'expert', split_axis=0...  157 us
    all_to_all x1, waiting for transfers between devices, side_by_side(): lax.all_to_all(both, axis, split_axis=split_dim, concat_axis=concat_dim,...  103 us
    all_to_all x1, blocking collectives, cut_exchange(): lax.all_to_all(section, axis, split_axis=0, concat_axis=0, tiled=True)  55.1 us
    ppermute x2, waiting for transfers between devices, from_behind(): return lax.ppermute(value, axis, pairs)  41.7 us
    all_to_all x2, starting transfers between devices, send_rows(): lax.all_to_all(jnp.repeat(buffer, slices, axis=0), 'expert', split_axis=0...  16.8 us
    reshape x2, local copies, waits for them, and re-layouts, send_rows(): return received.reshape(ndev * capacity, width)  16.2 us
    all_to_all x1, waiting for transfers between devices, cut_exchange(): lax.all_to_all(section, axis, split_axis=0, concat_axis=0, tiled=True)  12.1 us
  transfers between devices with their start and end apart: 6, of which 6 were waited for; matrix products, arithmetic and copies ran while one was open for 18% of the time, Pallas kernels for 0%

commit v1 on v0

v1 whole, which is shorter than its diff:
```python
import jax
import jax.numpy as jnp
from jax import lax
from jax.sharding import Mesh, PartitionSpec as P

CAP = 10
TOK = 128
D = 7168
HALF = D // 2
F = 128
ROWS = (16, 24)
UP = [(i, (i + 1) % 4) for i in range(4)]
DN = [(i, (i - 1) % 4) for i in range(4)]
OFFS = (0, -1, 1, 2)
f32 = jnp.float32
bf16 = jnp.bfloat16


def ring_gather(x, axis):
    left = lax.ppermute(x, axis, UP)
    right = lax.ppermute(x, axis, DN)
    h = x.shape[-1] // 2
    far_a = lax.ppermute(left[..., :h], axis, UP)
    far_b = lax.ppermute(right[..., h:], axis, DN)
    return [x, left, right, jnp.concatenate([far_a, far_b], -1)]


def ring_scatter(parts, axis):
    own, left, right, far = parts
    h = (own.shape[-1] // 256) * 128
    far_a = lax.ppermute(far[..., :h], axis, DN)
    far_b = lax.ppermute(far[..., h:], axis, UP)
    left = jnp.concatenate(
        [(left[..., :h].astype(f32) + far_a.astype(f32)).astype(bf16), left[..., h:]], -1
    )
    right = jnp.concatenate(
        [right[..., :h], (right[..., h:].astype(f32) + far_b.astype(f32)).astype(bf16)], -1
    )
    from_right = lax.ppermute(left, axis, DN)
    from_left = lax.ppermute(right, axis, UP)
    return (own.astype(f32) + from_right.astype(f32) + from_left.astype(f32)).astype(bf16)


def routing(ids, gates):
    expert_ids = jnp.arange(2, dtype=jnp.int32)
    matches = ids[None, :, :] == expert_ids[:, None, None]
    routed = jnp.any(matches, axis=2)
    weights = jnp.sum(jnp.where(matches, gates[None, :, :], 0.0), axis=2)
    position = jnp.cumsum(routed.astype(jnp.int32), axis=1) - 1
    slot_ids = jnp.arange(CAP, dtype=jnp.int32)
    placing = (position[:, None, :] == slot_ids[None, :, None]) & routed[:, None, :]
    return matches, placing.astype(f32), weights


def own_other(pair, z):
    own = jnp.where(z == 0, pair[0], pair[1])
    other = jnp.where(z == 0, pair[1], pair[0])
    return own, other


def slot_index(z, x, y):
    offs = jnp.array(OFFS, jnp.int32)
    block = ((x + offs) % 4)[None, :] * 4 + ((y + offs) % 4)[:, None]
    own = (z * 16 + block) * CAP
    other = ((1 - z) * 16 + block) * CAP
    far = jnp.full((4, 4, CAP), -1, jnp.int32)
    rank = jnp.arange(CAP, dtype=jnp.int32)
    first = jnp.concatenate([far, own[..., None] + rank[:6]], -1)
    second = jnp.concatenate([own[..., None] + rank[6:], far, other[..., None] + rank], -1)
    return first, second


def expert_rows(gathered_a, gathered_b, w1, w2, pre, is_fwd, lane):
    rows = is_fwd.shape[0]
    xa = jnp.stack(gathered_a).reshape(16 * rows, HALF)
    xb = jnp.stack(gathered_b).reshape(16 * rows, HALF)
    za = jnp.dot(xa, w1[:HALF], preferred_element_type=f32)
    zb = jnp.dot(xb, w1[HALF:], preferred_element_type=f32)
    zb = zb.reshape(4, 4, rows, 384).transpose(1, 0, 2, 3)
    z = za.reshape(4, 4, rows, 384) + zb
    fwd = is_fwd[None, None, :, None]
    hidden = jax.nn.silu(z[..., :F]) * z[..., F : 2 * F]
    g = pre[..., :F]
    u = pre[..., F:]
    grad_hidden = z[..., 2 * F :]
    s = jax.nn.sigmoid(g)
    activated = g * s
    dots = jnp.sum(grad_hidden * activated * u, axis=-1, keepdims=True)
    grad_gate = grad_hidden * u * s * (1.0 + g * (1.0 - s))
    grad_up = grad_hidden * activated
    h = jnp.concatenate(
        [
            jnp.where(fwd, hidden, 0.0),
            jnp.where(fwd, 0.0, grad_gate),
            jnp.where(fwd, 0.0, grad_up),
        ],
        -1,
    ).astype(bf16)
    h_t = h.transpose(1, 0, 2, 3)
    out_a = jnp.dot(h.reshape(16 * rows, 384), w2[:, :HALF], preferred_element_type=f32)
    out_b = jnp.dot(h_t.reshape(16 * rows, 384), w2[:, HALF:], preferred_element_type=f32)
    lanes = jnp.arange(128) == lane
    dots = jnp.where(lanes, jnp.where(fwd, 0.0, dots), 0.0).astype(bf16)
    out_a = out_a.astype(bf16).reshape(4, 4, rows, HALF)
    out_b = out_b.astype(bf16).reshape(4, 4, rows, HALF)
    out_b = jnp.concatenate([out_b, dots.transpose(1, 0, 2, 3)], -1)
    return out_a, out_b


def body(
    act_in, cotangent, fwd_ids, fwd_gates, bwd_ids, bwd_gates,
    gate_w, up_w, down_w, gate_pre, up_pre,
):
    z = lax.axis_index("z")
    x = lax.axis_index("x")
    y = lax.axis_index("y")
    matches_f, placing_f, weights_f = routing(fwd_ids[0], fwd_gates[0])
    matches_b, placing_b, weights_b = routing(bwd_ids[0], bwd_gates[0])
    own_f, other_f = own_other(placing_f, z)
    own_b, other_b = own_other(placing_b, z)
    none = jnp.zeros_like(own_f)
    pick_f = jnp.concatenate([own_f, none, other_f, none]).astype(bf16)
    pick_b = jnp.concatenate([none, own_b, none, other_b]).astype(bf16)
    rows = jnp.dot(pick_f, act_in[0], preferred_element_type=f32) + jnp.dot(
        pick_b, cotangent[0], preferred_element_type=f32
    )
    rows = rows.astype(bf16)
    first = rows[:16]
    swapped = lax.ppermute(rows[16:], "z", [(0, 1), (1, 0)])
    second = jnp.where(jnp.arange(24)[:, None] < 4, rows[16:], swapped)

    scale_f = lax.ppermute(
        (placing_f * weights_f[:, None, :]).reshape(2 * CAP, TOK), "section",
        [(i, (i + 1) % 8) for i in range(8)],
    )
    scale_b = lax.ppermute(
        (placing_b * weights_b[:, None, :]).reshape(2 * CAP, TOK), "section",
        [(i, (i - 1) % 8) for i in range(8)],
    )

    w1 = jnp.concatenate([gate_w[0], up_w[0], down_w[0].T], 1)
    w2 = jnp.concatenate([down_w[0], gate_w[0].T, up_w[0].T], 0)
    pre = jnp.concatenate([gate_pre[0], up_pre[0]], 1)
    slots = jnp.arange(pre.shape[0], dtype=jnp.int32)
    results = []
    for chunk, index, n in zip((first, second), slot_index(z, x, y), ROWS):
        pick = (index[..., None] == slots).astype(bf16)
        pre_rows = jnp.einsum("abrs,sf->abrf", pick, pre, preferred_element_type=f32)
        ga = ring_gather(jnp.stack(ring_gather(chunk[:, :HALF], "x")), "y")
        gb = ring_gather(jnp.stack(ring_gather(chunk[:, HALF:], "y")), "x")
        row = jnp.arange(n)
        is_fwd = row < CAP if n == 16 else (row >= 4) & (row < 14)
        oa, ob = expert_rows(ga, gb, w1, w2, pre_rows, is_fwd, x * 4 + y)
        ra = ring_scatter([oa[k] for k in range(4)], "y")
        rb = ring_scatter([ob[k] for k in range(4)], "x")
        ra = ring_scatter([ra[k] for k in range(4)], "x")
        rb = ring_scatter([rb[k] for k in range(4)], "y")
        results.append((ra, rb[:, :HALF], rb[:, HALF:]))
    (a0, b0, d0), (a1, b1, d1) = results

    def hop(a, b, step, flip):
        both = jnp.concatenate([a, b], 0)
        pairs = []
        for s in range(8):
            for zz in range(2):
                pairs.append((s * 2 + zz, (s + step) % 8 * 2 + (zz ^ flip)))
        out = lax.ppermute(both, ("section", "z"), pairs)
        return jnp.concatenate([out[:CAP], out[CAP:]], 1)

    fo = hop(a0[:10], b0[:10], 1, 0)
    bo = hop(jnp.concatenate([a0[10:], a1[:4]], 0), jnp.concatenate([b0[10:], b1[:4]], 0), -1, 0)
    fx = hop(a1[4:14], b1[4:14], 1, 1)
    bx = hop(a1[14:], b1[14:], -1, 1)

    def place(own, other, scale):
        r = jnp.where(z == 0, jnp.concatenate([own, other], 0), jnp.concatenate([other, own], 0))
        out = jnp.einsum("rt,rd->td", scale, r.astype(f32), precision=lax.Precision.HIGHEST)
        return out.astype(bf16)[None]

    next_act = place(fo, fx, scale_f)
    prev_grad = place(bo, bx, scale_b)

    dots0 = jnp.sum(d0.astype(f32), axis=1, keepdims=True)
    dots1 = jnp.sum(d1.astype(f32), axis=1, keepdims=True)
    dots_own = jnp.concatenate([dots0[10:], dots1[:4]], 0)
    dots_send = jnp.broadcast_to(dots1[14:], (CAP, 128))
    dots_other = lax.ppermute(dots_send, "z", [(0, 1), (1, 0)])[:, :1]
    dots = jnp.stack(
        [jnp.where(z == 0, dots_own, dots_other), jnp.where(z == 0, dots_other, dots_own)]
    )
    token_dots = jnp.sum(placing_b * dots, axis=1)
    gate_grad = jnp.sum(jnp.where(matches_b, token_dots[:, :, None], 0.0), axis=0)
    return next_act, prev_grad, gate_grad[None]


def solution(mesh):
    grid = Mesh(mesh.devices.reshape(8, 2, 4, 4), ("section", "z", "x", "y"))
    ex = ("z", "x", "y")
    tok = P("section", ex, None)
    col = P("section", None, ex)
    in_specs = (tok, tok, tok, tok, tok, tok, col, col, tok, col, col)
    return jax.shard_map(
        body, mesh=grid, in_specs=in_specs, out_specs=(tok, tok, tok), check_vma=False
    )
```

time: 528 us -> 274 us (0.52)
  waiting for transfers between devices: 314 us -> 83.7 us
  starting transfers between devices: 40 us -> 132 us
  blocking collectives: 55.1 us -> 0 us
  local copies, waits for them, and re-layouts: 55.7 us -> 12.3 us
  matrix products: 34.7 us -> 19.6 us
    all_to_all x4 -> x0, waiting for transfers between devices: 272 us -> none  [the longest x2 157 us: send_rows(): lax.all_to_all(jnp.repeat(buffer, slices, axis=0), 'expert', split_axis=0...]
    ppermute x2 -> x72, starting transfers between devices: 8.47 us -> 132 us  [the longest x4 37.7 us: hop(): out = lax.ppermute(both, ('section', 'z'), pairs)]
    all_to_all x1 -> x0, blocking collectives: 55.1 us -> none  [cut_exchange(): lax.all_to_all(section, axis, split_axis=0, concat_axis=0, tiled=True)]
    ppermute x2 -> x72, waiting for transfers between devices: 41.7 us -> 83.7 us  [the longest x8 18.8 us: ring_scatter(): from_right = lax.ppermute(left, axis, DN)]
    all_to_all x4 -> x0, starting transfers between devices: 31.5 us -> none  [the longest x2 16.8 us: send_rows(): lax.all_to_all(jnp.repeat(buffer, slices, axis=0), 'expert', split_axis=0...]
    reshape x3 -> x0, local copies, waits for them, and re-layouts: 24 us -> none  [the longest x2 16.2 us: send_rows(): return received.reshape(ndev * capacity, width)]
    dot_general x10 -> x14, matrix products: 34.7 us -> 19.6 us  [the longest x2 5.74 us: place(): jnp.einsum('rt,rd->td', scale, r.astype(f32), precision=lax.Precision.HIG...]
    split x3 -> x0, local copies, waits for them, and re-layouts: 11.5 us -> none  [the longest x1 6.71 us: cut_exchange(): jnp.split(blocks, edges_of(blocks.shape[cut], pieces), axis=cut)]
  transfers between devices with their start and end apart: 6 -> 72, of which waited for: 6 -> 25; matrix products, arithmetic and copies ran while one was open for 18% -> 16% of each run, Pallas kernels for 0% -> 0%
where the time goes in v1:
time: 274 us; the launch traced here: 270 us
  starting transfers between devices  132 us (48%)
  waiting for transfers between devices  83.7 us (31%)
  other arithmetic  19.9 us (7%)
  matrix products  19.6 us (7%)
  local copies, waits for them, and re-layouts  12.3 us (4%)
    ppermute x4, starting transfers between devices, hop(): out = lax.ppermute(both, ('section', 'z'), pairs)  37.7 us
    ppermute x8, starting transfers between devices, ring_gather(): far_b = lax.ppermute(right[..., h:], axis, DN)  28.9 us
    ppermute x8, waiting for transfers between devices, ring_scatter(): from_right = lax.ppermute(left, axis, DN)  18.8 us
    ppermute x8, starting transfers between devices, ring_scatter(): far_a = lax.ppermute(far[..., :h], axis, DN)  18.2 us
    ppermute x8, waiting for transfers between devices, ring_scatter(): far_b = lax.ppermute(far[..., h:], axis, UP)  17.3 us
    ppermute x8, starting transfers between devices, ring_scatter(): from_right = lax.ppermute(left, axis, DN)  13.5 us
    ppermute x8, starting transfers between devices, ring_gather(): right = lax.ppermute(x, axis, DN)  11.2 us
    ppermute x8, waiting for transfers between devices, ring_scatter(): from_left = lax.ppermute(right, axis, UP)  11.1 us
  transfers between devices with their start and end apart: 72, of which 25 were waited for; matrix products, arithmetic and copies ran while one was open for 16% of the time, Pallas kernels for 0%

profile of v1, /device:TPU:1, one launch (start us, length us, event | category | flops | bytes accessed | tf_op | source)
XLA Modules:
  0.0 269.9 jit_solution(15929297368453831423)
XLA Ops:
  14.2 3.3 %copy.42 = bf16[1,128,7168]{1,2,0:T(8,128)(2,1)S(1)} copy(bf16[1,128,7168]{2,1,0:T(8,128)(2,1)} %param.20) | data formatting | bytes 3670016 | tf_op args[8]
  20.3 5.9 %pad_maximum_fusion = bf16[7168,384]{1,0:T(8,128)(2,1)} fusion(bf16[7168,128]{1,0:T(8,128)(2,1)S(1)} %bitcast.219, bf16[7168,128]{1,0:T(8,128)(2,1)} %bitcast.225, bf16[7168,128]{1,0:T(8,128)(2,1)} %bitcast.227), kind=kLoop, calls=%fused_computation.8 | loop fusion | flops 16515072 | bytes 11010048 | tf_op jit(solution)/shard_map/concatenate | solution.py:141
  26.2 3.0 %pad_maximum_fusion.1 = bf16[384,7168]{0,1:T(8,128)(2,1)} fusion(bf16[128,7168]{0,1:T(8,128)(2,1)S(1)} %bitcast.226, bf16[128,7168]{0,1:T(8,128)(2,1)S(1)} %bitcast.228, bf16[128,7168]{0,1:T(8,128)(2,1)S(1)} %bitcast.220), kind=kLoop, calls=%fused_computation.9 | loop fusion | flops 16515072 | bytes 11010048 | tf_op jit(solution)/shard_map/concatenate | solution.py:142
  35.2 2.7 collective-permute-start.4
  40.5 2.7 collective-permute-start.36
  43.6 2.7 collective-permute-start.44
  46.2 6.8 %collective-permute-done.35 = bf16[24,3584]{1,0:T(8,128)(2,1)S(1)} collective-permute-done((bf16[24,3584]{1,0:T(8,128)(2,1)S(1)}, bf16[24,3584]{1,0:T(8,128)(2,1)S(1)}, u32[]{:S(2)}, u32[]{:S(2)}) %collective-permute-start.35) | collective-permute-done | bytes 172064 | tf_op jit(solution)/shard_map/ppermute | solution.py:20
  53.1 2.7 %collective-permute-start.38 = (bf16[24,1792]{1,0:T(8,128)(2,1)S(1)}, bf16[24,1792]{1,0:T(8,128)(2,1)S(1)}, u32[]{:S(2)}, u32[]{:S(2)}) collective-permute-start(bf16[24,1792]{1,0:T(8,128)(2,1)S(1)} %slice.688), channel_id=1, source_target_pairs={{0,12},{4,0},{8,4},{12,8},{1,13},{5,1},{9,5},{13,9},{2,14},{6,2},{... | collective-permute-start | bytes 258056 | tf_op jit(solution)/shard_map/ppermute | solution.py:24
  57.7 2.7 collective-permute-start.46
  60.5 7.2 %collective-permute-done.45 = bf16[24,1792]{1,0:T(8,128)(2,1)S(1)} collective-permute-done((bf16[24,1792]{1,0:T(8,128)(2,1)S(1)}, bf16[24,1792]{1,0:T(8,128)(2,1)S(1)}, u32[]{:S(2)}, u32[]{:S(2)}) %collective-permute-start.45) | collective-permute-done | bytes 86048 | tf_op jit(solution)/shard_map/ppermute | solution.py:23
  76.3 11.3 %collective-permute-start.8 = (bf16[4,16,1792]{2,1,0:T(8,128)(2,1)S(1)}, bf16[4,16,1792]{2,1,0:T(8,128)(2,1)S(1)}, u32[]{:S(2)}, u32[]{:S(2)}) collective-permute-start(bf16[4,16,1792]{2,1,0:T(8,128)(2,1)S(1)} %slice.624), channel_id=1, source_target_pairs={{0,3},{1,0},{2,1},{3,2},{4,7},{5,4},{6,5},{7,6},{8,11},{9,8},{10,9... | collective-permute-start | bytes 688136 | tf_op jit(solution)/shard_map/ppermute | solution.py:24
  97.0 3.5 %collective-permute-start.17 = (bf16[4,16,1792]{2,1,0:T(8,128)(2,1)S(1)}, bf16[4,16,1792]{2,1,0:T(8,128)(2,1)S(1)}, u32[]{:S(2)}, u32[]{:S(2)}) collective-permute-start(bf16[4,16,1792]{2,1,0:T(8,128)(2,1)S(1)} %get-tuple-element.48), channel_id=1, source_target_pairs={{0,3},{1,0},{2,1},{3,2},{4,7},{5,4},{6,5},{7,6},{8,11},{9,8},{10,9... | collective-permute-start | bytes 688136 | tf_op jit(solution)/shard_map/ppermute | solution.py:31
  105.7 5.7 %collective-permute-done.19 = bf16[4,16,1792]{2,1,0:T(8,128)(2,1)S(1)} collective-permute-done((bf16[4,16,1792]{2,1,0:T(8,128)(2,1)S(1)}, bf16[4,16,1792]{2,1,0:T(8,128)(2,1)S(1)}, u32[]{:S(2)}, u32[]{:S(2)}) %collective-permute-start.19) | collective-permute-done | bytes 229408 | tf_op jit(solution)/shard_map/ppermute | solution.py:32
  113.9 2.9 %collective-permute-done.25 = bf16[4,16,1792]{2,1,0:T(8,128)(2,1)S(1)} collective-permute-done((bf16[4,16,1792]{2,1,0:T(8,128)(2,1)S(1)}, bf16[4,16,1792]{2,1,0:T(8,128)(2,1)S(1)}, u32[]{:S(2)}, u32[]{:S(2)}) %collective-permute-start.25) | collective-permute-done | bytes 229408 | tf_op jit(solution)/shard_map/ppermute | solution.py:31
  116.9 6.9 %collective-permute-done.27 = bf16[4,16,1920]{2,1,0:T(8,128)(2,1)S(1)} collective-permute-done((bf16[4,16,1920]{2,1,0:T(8,128)(2,1)S(1)}, bf16[4,16,1920]{2,1,0:T(8,128)(2,1)S(1)}, u32[]{:S(2)}, u32[]{:S(2)}) %collective-permute-start.27) | collective-permute-done | bytes 245792 | tf_op jit(solution)/shard_map/ppermute | solution.py:32
  127.8 3.6 %collective-permute-done.18 = bf16[4,16,3584]{2,1,0:T(8,128)(2,1)S(1)} collective-permute-done((bf16[4,16,3584]{2,1,0:T(8,128)(2,1)S(1)}, bf16[4,16,3584]{2,1,0:T(8,128)(2,1)S(1)}, u32[]{:S(2)}, u32[]{:S(2)}) %collective-permute-start.18) | collective-permute-done | bytes 458784 | tf_op jit(solution)/shard_map/ppermute | solution.py:39
  135.5 2.9 %collective-permute-start.50 = (bf16[4,24,1792]{2,1,0:T(8,128)(2,1)S(1)}, bf16[4,24,1792]{2,1,0:T(8,128)(2,1)S(1)}, u32[]{:S(2)}, u32[]{:S(2)}) collective-permute-start(bf16[4,24,1792]{2,1,0:T(8,128)(2,1)S(1)} %slice.695), channel_id=1, source_target_pairs={{0,12},{4,0},{8,4},{12,8},{1,13},{5,1},{9,5},{13,9},{2,14},{6,2},{... | collective-permute-start | bytes 1032200 | tf_op jit(solution)/shard_map/ppermute | solution.py:24
  138.7 4.5 %collective-permute-done.21 = bf16[16,1792]{1,0:T(8,128)(2,1)S(1)} collective-permute-done((bf16[16,1792]{1,0:T(8,128)(2,1)S(1)}, bf16[16,1792]{1,0:T(8,128)(2,1)S(1)}, u32[]{:S(2)}, u32[]{:S(2)}) %collective-permute-start.21) | collective-permute-done | bytes 57376 | tf_op jit(solution)/shard_map/ppermute | solution.py:31
  143.2 4.6 %collective-permute-done.23 = bf16[16,1792]{1,0:T(8,128)(2,1)S(1)} collective-permute-done((bf16[16,1792]{1,0:T(8,128)(2,1)S(1)}, bf16[16,1792]{1,0:T(8,128)(2,1)S(1)}, u32[]{:S(2)}, u32[]{:S(2)}) %collective-permute-start.23) | collective-permute-done | bytes 57376 | tf_op jit(solution)/shard_map/ppermute | solution.py:32
  162.7 2.7 %collective-permute-start.59 = (bf16[4,24,1792]{2,1,0:T(8,128)(2,1)S(1)}, bf16[4,24,1792]{2,1,0:T(8,128)(2,1)S(1)}, u32[]{:S(2)}, u32[]{:S(2)}) collective-permute-start(bf16[4,24,1792]{2,1,0:T(8,128)(2,1)S(1)} %slice.729), channel_id=1, source_target_pairs={{0,12},{4,0},{8,4},{12,8},{1,13},{5,1},{9,5},{13,9},{2,14},{6,2},{... | collective-permute-start | bytes 1032200 | tf_op jit(solution)/shard_map/ppermute | solution.py:31
  165.5 2.7 %collective-permute-start.30 = (bf16[16,3712]{1,0:T(8,128)(2,1)S(1)}, bf16[16,3712]{1,0:T(8,128)(2,1)S(1)}, u32[]{:S(2)}, u32[]{:S(2)}) collective-permute-start(bf16[16,3712]{1,0:T(8,128)(2,1)S(1)} %pad_maximum_fusion.26), channel_id=1, source_target_pairs={{0,3},{1,0},{2,1},{3,2},{4,7},{5,4},{6,5},{7,6},{8,11},{9,8},{10,9... | collective-permute-start | bytes 356360 | tf_op jit(solution)/shard_map/ppermute | solution.py:39
  170.0 3.1 %collective-permute-done.32 = bf16[16,3712]{1,0:T(8,128)(2,1)S(1)} collective-permute-done((bf16[16,3712]{1,0:T(8,128)(2,1)S(1)}, bf16[16,3712]{1,0:T(8,128)(2,1)S(1)}, u32[]{:S(2)}, u32[]{:S(2)}) %collective-permute-start.32) | collective-permute-done | bytes 118816 | tf_op jit(solution)/shard_map/ppermute | solution.py:40
  173.4 27.0 %collective-permute-start.33 = (bf16[20,3584]{1,0:T(8,128)(2,1)S(1)}, bf16[20,3584]{1,0:T(8,128)(2,1)S(1)}, u32[]{:S(2)}, u32[]{:S(2)}) collective-permute-start(bf16[20,3584]{1,0:T(8,128)(2,1)S(1)} %pad_maximum_fusion.20), channel_id=1, source_target_pairs={{0,32},{16,48},{32,64},{48,80},{64,96},{80,112},{96,128},{112,144}... | collective-permute-start | bytes 430088 | tf_op jit(solution)/shard_map/ppermute | solution.py:167
  206.8 11.5 %collective-permute-done.52 = bf16[4,24,3584]{2,1,0:T(8,128)(2,1)S(1)} collective-permute-done((bf16[4,24,3584]{2,1,0:T(8,128)(2,1)S(1)}, bf16[4,24,3584]{2,1,0:T(8,128)(2,1)S(1)}, u32[]{:S(2)}, u32[]{:S(2)}) %collective-permute-start.52) | collective-permute-done | bytes 688160 | tf_op jit(solution)/shard_map/ppermute | solution.py:39
  227.8 3.0 %collective-permute-start.64 = (bf16[24,3712]{1,0:T(8,128)(2,1)S(1)}, bf16[24,3712]{1,0:T(8,128)(2,1)S(1)}, u32[]{:S(2)}, u32[]{:S(2)}) collective-permute-start(bf16[24,3712]{1,0:T(8,128)(2,1)S(1)} %pad_maximum_fusion.18), channel_id=1, source_target_pairs={{0,3},{1,0},{2,1},{3,2},{4,7},{5,4},{6,5},{7,6},{8,11},{9,8},{10,9... | collective-permute-start | bytes 534536 | tf_op jit(solution)/shard_map/ppermute | solution.py:39
  234.0 3.8 %collective-permute-done.66 = bf16[24,3712]{1,0:T(8,128)(2,1)S(1)} collective-permute-done((bf16[24,3712]{1,0:T(8,128)(2,1)S(1)}, bf16[24,3712]{1,0:T(8,128)(2,1)S(1)}, u32[]{:S(2)}, u32[]{:S(2)}) %collective-permute-start.66) | collective-permute-done | bytes 178208 | tf_op jit(solution)/shard_map/ppermute | solution.py:40
  238.2 6.4 %collective-permute-start.69 = (bf16[20,3584]{1,0:T(8,128)(2,1)S(1)}, bf16[20,3584]{1,0:T(8,128)(2,1)S(1)}, u32[]{:S(2)}, u32[]{:S(2)}) collective-permute-start(bf16[20,3584]{1,0:T(8,128)(2,1)S(1)} %pad_maximum_fusion.24), channel_id=1, source_target_pairs={{0,224},{16,240},{32,0},{48,16},{64,32},{80,48},{96,64},{112,80},{... | collective-permute-start | bytes 430088 | tf_op jit(solution)/shard_map/ppermute | solution.py:167
  246.2 3.5 %collective-permute-start.67 = (bf16[20,3584]{1,0:T(8,128)(2,1)S(1)}, bf16[20,3584]{1,0:T(8,128)(2,1)S(1)}, u32[]{:S(2)}, u32[]{:S(2)}) collective-permute-start(bf16[20,3584]{1,0:T(8,128)(2,1)S(1)} %pad_maximum_fusion.23), channel_id=1, source_target_pairs={{0,48},{16,32},{32,80},{48,64},{64,112},{80,96},{96,144},{112,128}... | collective-permute-start | bytes 430088 | tf_op jit(solution)/shard_map/ppermute | solution.py:167
  249.7 4.3 %collective-permute-done.71 = f32[10,128]{0,1:T(8,128)S(1)} collective-permute-done((f32[10,128]{0,1:T(8,128)S(1)}, f32[10,128]{0,1:T(8,128)S(1)}, u32[]{:S(2)}, u32[]{:S(2)}) %collective-permute-start.71) | collective-permute-done | bytes 5152 | tf_op jit(solution)/shard_map/ppermute | solution.py:187
  257.0 5.6 %collective-permute-start = (f32[20,128]{1,0:T(8,128)S(1)}, f32[20,128]{1,0:T(8,128)S(1)}, u32[]{:S(2)}, u32[]{:S(2)}) collective-permute-start(f32[20,128]{1,0:T(8,128)S(1)} %get-tuple-element.84), channel_id=1, source_target_pairs={{0,32},{32,64},{64,96},{96,128},{128,160},{160,192},{192,224},{224... | collective-permute-start | bytes 30728 | tf_op jit(solution)/shard_map/ppermute | solution.py:132
  263.9 2.9 %fusion.1 = bf16[1,128,7168]{2,1,0:T(8,128)(2,1)} fusion(f32[20,128]{1,0:T(8,128)S(1)} %collective-permute-done.68, bf16[10,3584]{1,0:T(8,128)(2,1)S(1)} %get-tuple-element.64, bf16[10,3584]{1,0:T(8,128)(2,1)S(1)} %get-tuple-element.63, bf16[10,3584]{1,0:T(8,128)(2,1)S(1)} %get-tuple-element.62, bf16[10,3584]{1,0:T(8,128)(2,1)S(1)} %get-tuple-element.61, ...), kind=kOutput, calls=%fused_computation.3 | convolution fusion | flops 223555584 | bytes 2131969 | tf_op jit(solution)/shard_map/rt,rd->td/dot_general | solution.py:177
  266.8 2.9 %fusion = bf16[1,128,7168]{2,1,0:T(8,128)(2,1)} fusion(f32[20,128]{1,0:T(8,128)S(1)} %collective-permute-done, bf16[10,3584]{1,0:T(8,128)(2,1)S(1)} %get-tuple-element.70, bf16[10,3584]{1,0:T(8,128)(2,1)S(1)} %get-tuple-element.69, bf16[10,3584]{1,0:T(8,128)(2,1)S(1)} %get-tuple-element.68, bf16[10,3584]{1,0:T(8,128)(2,1)S(1)} %get-tuple-element.67, ...), kind=kOutput, calls=%fused_computation.2 | convolution fusion | flops 223555584 | bytes 2131969 | tf_op jit(solution)/shard_map/rt,rd->td/dot_general | solution.py:177
  (362 shorter events, 102.6 us)
Async XLA Ops:
  5.6 24.4 %collective-permute-start.9 = (bf16[16,3584]{1,0:T(8,128)(2,1)}, bf16[16,3584]{1,0:T(8,128)(2,1)}, u32[]{:S(2)}, u32[]{:S(2)}) collective-permute-start(bf16[16,3584]{1,0:T(8,128)(2,1)} %get-tuple-element.40), channel_id=1, source_target_pairs={{0,1},{1,2},{2,3},{3,0},{4,5},{5,6},{6,7},{7,4},{8,9},{9,10},{10,1... | collective-permute-start | bytes 344072 | tf_op jit(solution)/shard_map/ppermute | solution.py:20
  7.7 23.1 %collective-permute-start.10 = (bf16[16,3584]{1,0:T(8,128)(2,1)}, bf16[16,3584]{1,0:T(8,128)(2,1)}, u32[]{:S(2)}, u32[]{:S(2)}) collective-permute-start(bf16[16,3584]{1,0:T(8,128)(2,1)} %get-tuple-element.40), channel_id=1, source_target_pairs={{0,3},{1,0},{2,1},{3,2},{4,7},{5,4},{6,5},{7,6},{8,11},{9,8},{10,9... | collective-permute-start | bytes 344072 | tf_op jit(solution)/shard_map/ppermute | solution.py:21
  9.1 25.2 %collective-permute-start.1 = (bf16[16,3584]{1,0:T(8,128)(2,1)}, bf16[16,3584]{1,0:T(8,128)(2,1)S(1)}, u32[]{:S(2)}, u32[]{:S(2)}) collective-permute-start(bf16[16,3584]{1,0:T(8,128)(2,1)} %get-tuple-element.41), channel_id=1, source_target_pairs={{0,4},{4,8},{8,12},{12,0},{1,5},{5,9},{9,13},{13,1},{2,6},{6,10},{... | collective-permute-start | bytes 344072 | tf_op jit(solution)/shard_map/ppermute | solution.py:20
  10.3 24.1 %collective-permute-start.2 = (bf16[16,3584]{1,0:T(8,128)(2,1)}, bf16[16,3584]{1,0:T(8,128)(2,1)}, u32[]{:S(2)}, u32[]{:S(2)}) collective-permute-start(bf16[16,3584]{1,0:T(8,128)(2,1)} %get-tuple-element.41), channel_id=1, source_target_pairs={{0,12},{4,0},{8,4},{12,8},{1,13},{5,1},{9,5},{13,9},{2,14},{6,2},{... | collective-permute-start | bytes 344072 | tf_op jit(solution)/shard_map/ppermute | solution.py:21
  12.6 26.6 %collective-permute-start.34 = (bf16[24,7168]{1,0:T(8,128)(2,1)}, bf16[24,7168]{1,0:T(8,128)(2,1)}, u32[]{:S(2)}, u32[]{:S(2)}) collective-permute-start(bf16[24,7168]{1,0:T(8,128)(2,1)} %slice.685), channel_id=1, source_target_pairs={{0,16},{16,0},{1,17},{17,1},{2,18},{18,2},{3,19},{19,3},{4,20},{20... | collective-permute-start | bytes 1032200 | tf_op jit(solution)/shard_map/ppermute | solution.py:129
  39.1 30.0 %collective-permute-start.13 = (bf16[4,16,3584]{2,1,0:T(8,128)(2,1)S(1)}, bf16[4,16,3584]{2,1,0:T(8,128)(2,1)S(1)}, u32[]{:S(2)}, u32[]{:S(2)}) collective-permute-start(bf16[4,16,3584]{2,1,0:T(8,128)(2,1)S(1)} %get-tuple-element.53), channel_id=1, source_target_pairs={{0,4},{4,8},{8,12},{12,0},{1,5},{5,9},{9,13},{13,1},{2,6},{6,10},{... | collective-permute-start | bytes 1376264 | tf_op jit(solution)/shard_map/ppermute | solution.py:20
  43.2 13.7 %collective-permute-start.43 = (bf16[24,3584]{1,0:T(8,128)(2,1)S(1)}, bf16[24,3584]{1,0:T(8,128)(2,1)S(1)}, u32[]{:S(2)}, u32[]{:S(2)}) collective-permute-start(bf16[24,3584]{1,0:T(8,128)(2,1)S(1)} %get-tuple-element.57), channel_id=1, source_target_pairs={{0,1},{1,2},{2,3},{3,0},{4,5},{5,6},{6,7},{7,4},{8,9},{9,10},{10,1... | collective-permute-start | bytes 516104 | tf_op jit(solution)/shard_map/ppermute | solution.py:20
  57.0 15.1 %collective-permute-start.5 = (bf16[4,16,3584]{2,1,0:T(8,128)(2,1)S(1)}, bf16[4,16,3584]{2,1,0:T(8,128)(2,1)S(1)}, u32[]{:S(2)}, u32[]{:S(2)}) collective-permute-start(bf16[4,16,3584]{2,1,0:T(8,128)(2,1)S(1)} %get-tuple-element.51), channel_id=1, source_target_pairs={{0,1},{1,2},{2,3},{3,0},{4,5},{5,6},{6,7},{7,4},{8,9},{9,10},{10,1... | collective-permute-start | bytes 1376264 | tf_op jit(solution)/shard_map/ppermute | solution.py:20
  67.6 57.6 %collective-permute-start.39 = (bf16[4,24,3584]{2,1,0:T(8,128)(2,1)S(1)}, bf16[4,24,3584]{2,1,0:T(8,128)(2,1)S(1)}, u32[]{:S(2)}, u32[]{:S(2)}) collective-permute-start(bf16[4,24,3584]{2,1,0:T(8,128)(2,1)S(1)} %get-tuple-element.31), channel_id=1, source_target_pairs={{0,1},{1,2},{2,3},{3,0},{4,5},{5,6},{6,7},{7,4},{8,9},{9,10},{10,1... | collective-permute-start | bytes 2064392 | tf_op jit(solution)/shard_map/ppermute | solution.py:20
  72.1 53.3 %collective-permute-start.40 = (bf16[4,24,3584]{2,1,0:T(8,128)(2,1)S(1)}, bf16[4,24,3584]{2,1,0:T(8,128)(2,1)S(1)}, u32[]{:S(2)}, u32[]{:S(2)}) collective-permute-start(bf16[4,24,3584]{2,1,0:T(8,128)(2,1)S(1)} %get-tuple-element.31), channel_id=1, source_target_pairs={{0,3},{1,0},{2,1},{3,2},{4,7},{5,4},{6,5},{7,6},{8,11},{9,8},{10,9... | collective-permute-start | bytes 2064392 | tf_op jit(solution)/shard_map/ppermute | solution.py:21
  75.0 52.4 %collective-permute-start.47 = (bf16[4,24,3584]{2,1,0:T(8,128)(2,1)S(1)}, bf16[4,24,3584]{2,1,0:T(8,128)(2,1)S(1)}, u32[]{:S(2)}, u32[]{:S(2)}) collective-permute-start(bf16[4,24,3584]{2,1,0:T(8,128)(2,1)S(1)} %get-tuple-element.33), channel_id=1, source_target_pairs={{0,4},{4,8},{8,12},{12,0},{1,5},{5,9},{9,13},{13,1},{2,6},{6,10},{... | collective-permute-start | bytes 2064392 | tf_op jit(solution)/shard_map/ppermute | solution.py:20
  76.3 16.7 %collective-permute-start.8 = (bf16[4,16,1792]{2,1,0:T(8,128)(2,1)S(1)}, bf16[4,16,1792]{2,1,0:T(8,128)(2,1)S(1)}, u32[]{:S(2)}, u32[]{:S(2)}) collective-permute-start(bf16[4,16,1792]{2,1,0:T(8,128)(2,1)S(1)} %slice.624), channel_id=1, source_target_pairs={{0,3},{1,0},{2,1},{3,2},{4,7},{5,4},{6,5},{7,6},{8,11},{9,8},{10,9... | collective-permute-start | bytes 688136 | tf_op jit(solution)/shard_map/ppermute | solution.py:24
  88.7 38.7 %collective-permute-start.48 = (bf16[4,24,3584]{2,1,0:T(8,128)(2,1)S(1)}, bf16[4,24,3584]{2,1,0:T(8,128)(2,1)S(1)}, u32[]{:S(2)}, u32[]{:S(2)}) collective-permute-start(bf16[4,24,3584]{2,1,0:T(8,128)(2,1)S(1)} %get-tuple-element.33), channel_id=1, source_target_pairs={{0,12},{4,0},{8,4},{12,8},{1,13},{5,1},{9,5},{13,9},{2,14},{6,2},{... | collective-permute-start | bytes 2064392 | tf_op jit(solution)/shard_map/ppermute | solution.py:21
  127.5 25.8 %collective-permute-start.41 = (bf16[4,24,1792]{2,1,0:T(8,128)(2,1)S(1)}, bf16[4,24,1792]{2,1,0:T(8,128)(2,1)S(1)}, u32[]{:S(2)}, u32[]{:S(2)}) collective-permute-start(bf16[4,24,1792]{2,1,0:T(8,128)(2,1)S(1)} %slice.689), channel_id=1, source_target_pairs={{0,1},{1,2},{2,3},{3,0},{4,5},{5,6},{6,7},{7,4},{8,9},{9,10},{10,1... | collective-permute-start | bytes 1032200 | tf_op jit(solution)/shard_map/ppermute | solution.py:23
  131.4 22.4 %collective-permute-start.42 = (bf16[4,24,1792]{2,1,0:T(8,128)(2,1)S(1)}, bf16[4,24,1792]{2,1,0:T(8,128)(2,1)S(1)}, u32[]{:S(2)}, u32[]{:S(2)}) collective-permute-start(bf16[4,24,1792]{2,1,0:T(8,128)(2,1)S(1)} %slice.690), channel_id=1, source_target_pairs={{0,3},{1,0},{2,1},{3,2},{4,7},{5,4},{6,5},{7,6},{8,11},{9,8},{10,9... | collective-permute-start | bytes 1032200 | tf_op jit(solution)/shard_map/ppermute | solution.py:24
  133.9 16.1 %collective-permute-start.49 = (bf16[4,24,1792]{2,1,0:T(8,128)(2,1)S(1)}, bf16[4,24,1792]{2,1,0:T(8,128)(2,1)S(1)}, u32[]{:S(2)}, u32[]{:S(2)}) collective-permute-start(bf16[4,24,1792]{2,1,0:T(8,128)(2,1)S(1)} %slice.694), channel_id=1, source_target_pairs={{0,4},{4,8},{8,12},{12,0},{1,5},{5,9},{9,13},{13,1},{2,6},{6,10},{... | collective-permute-start | bytes 1032200 | tf_op jit(solution)/shard_map/ppermute | solution.py:23
  135.5 14.6 %collective-permute-start.50 = (bf16[4,24,1792]{2,1,0:T(8,128)(2,1)S(1)}, bf16[4,24,1792]{2,1,0:T(8,128)(2,1)S(1)}, u32[]{:S(2)}, u32[]{:S(2)}) collective-permute-start(bf16[4,24,1792]{2,1,0:T(8,128)(2,1)S(1)} %slice.695), channel_id=1, source_target_pairs={{0,12},{4,0},{8,4},{12,8},{1,13},{5,1},{9,5},{13,9},{2,14},{6,2},{... | collective-permute-start | bytes 1032200 | tf_op jit(solution)/shard_map/ppermute | solution.py:24
  147.9 14.7 %collective-permute-start.29 = (bf16[16,1792]{1,0:T(8,128)(2,1)S(1)}, bf16[16,1792]{1,0:T(8,128)(2,1)S(1)}, u32[]{:S(2)}, u32[]{:S(2)}) collective-permute-start(bf16[16,1792]{1,0:T(8,128)(2,1)S(1)} %slice.676), channel_id=1, source_target_pairs={{0,3},{1,0},{2,1},{3,2},{4,7},{5,4},{6,5},{7,6},{8,11},{9,8},{10,9... | collective-permute-start | bytes 172040 | tf_op jit(solution)/shard_map/ppermute | solution.py:31
  150.1 15.4 %collective-permute-start.22 = (bf16[16,3584]{1,0:T(8,128)(2,1)S(1)}, bf16[16,3584]{1,0:T(8,128)(2,1)S(1)}, u32[]{:S(2)}, u32[]{:S(2)}) collective-permute-start(bf16[16,3584]{1,0:T(8,128)(2,1)S(1)} %pad_maximum_fusion.28), channel_id=1, source_target_pairs={{0,12},{4,0},{8,4},{12,8},{1,13},{5,1},{9,5},{13,9},{2,14},{6,2},{... | collective-permute-start | bytes 344072 | tf_op jit(solution)/shard_map/ppermute | solution.py:39
  153.3 14.9 %collective-permute-start.24 = (bf16[16,3584]{1,0:T(8,128)(2,1)S(1)}, bf16[16,3584]{1,0:T(8,128)(2,1)S(1)}, u32[]{:S(2)}, u32[]{:S(2)}) collective-permute-start(bf16[16,3584]{1,0:T(8,128)(2,1)S(1)} %pad_maximum_fusion.29), channel_id=1, source_target_pairs={{0,4},{4,8},{8,12},{12,0},{1,5},{5,9},{9,13},{13,1},{2,6},{6,10},{... | collective-permute-start | bytes 344072 | tf_op jit(solution)/shard_map/ppermute | solution.py:40
  159.8 43.0 %collective-permute-start.51 = (bf16[4,24,1792]{2,1,0:T(8,128)(2,1)S(1)}, bf16[4,24,1792]{2,1,0:T(8,128)(2,1)S(1)}, u32[]{:S(2)}, u32[]{:S(2)}) collective-permute-start(bf16[4,24,1792]{2,1,0:T(8,128)(2,1)S(1)} %get-tuple-element.28), channel_id=1, source_target_pairs={{0,3},{1,0},{2,1},{3,2},{4,7},{5,4},{6,5},{7,6},{8,11},{9,8},{10,9... | collective-permute-start | bytes 1032200 | tf_op jit(solution)/shard_map/ppermute | solution.py:31
  162.5 40.5 %collective-permute-start.53 = (bf16[4,24,1792]{2,1,0:T(8,128)(2,1)S(1)}, bf16[4,24,1792]{2,1,0:T(8,128)(2,1)S(1)}, u32[]{:S(2)}, u32[]{:S(2)}) collective-permute-start(bf16[4,24,1792]{2,1,0:T(8,128)(2,1)S(1)} %get-tuple-element.29), channel_id=1, source_target_pairs={{0,1},{1,2},{2,3},{3,0},{4,5},{5,6},{6,7},{7,4},{8,9},{9,10},{10,1... | collective-permute-start | bytes 1032200 | tf_op jit(solution)/shard_map/ppermute | solution.py:32
  162.7 42.2 %collective-permute-start.59 = (bf16[4,24,1792]{2,1,0:T(8,128)(2,1)S(1)}, bf16[4,24,1792]{2,1,0:T(8,128)(2,1)S(1)}, u32[]{:S(2)}, u32[]{:S(2)}) collective-permute-start(bf16[4,24,1792]{2,1,0:T(8,128)(2,1)S(1)} %slice.729), channel_id=1, source_target_pairs={{0,12},{4,0},{8,4},{12,8},{1,13},{5,1},{9,5},{13,9},{2,14},{6,2},{... | collective-permute-start | bytes 1032200 | tf_op jit(solution)/shard_map/ppermute | solution.py:31
  170.0 36.3 %collective-permute-start.61 = (bf16[4,24,1920]{2,1,0:T(8,128)(2,1)S(1)}, bf16[4,24,1920]{2,1,0:T(8,128)(2,1)S(1)}, u32[]{:S(2)}, u32[]{:S(2)}) collective-permute-start(bf16[4,24,1920]{2,1,0:T(8,128)(2,1)S(1)} %slice.733), channel_id=1, source_target_pairs={{0,4},{4,8},{8,12},{12,0},{1,5},{5,9},{9,13},{13,1},{2,6},{6,10},{... | collective-permute-start | bytes 1105928 | tf_op jit(solution)/shard_map/ppermute | solution.py:32
  173.4 29.4 %collective-permute-start.33 = (bf16[20,3584]{1,0:T(8,128)(2,1)S(1)}, bf16[20,3584]{1,0:T(8,128)(2,1)S(1)}, u32[]{:S(2)}, u32[]{:S(2)}) collective-permute-start(bf16[20,3584]{1,0:T(8,128)(2,1)S(1)} %pad_maximum_fusion.20), channel_id=1, source_target_pairs={{0,32},{16,48},{32,64},{48,80},{64,96},{80,112},{96,128},{112,144}... | collective-permute-start | bytes 430088 | tf_op jit(solution)/shard_map/ppermute | solution.py:167
  202.9 15.4 %collective-permute-start.52 = (bf16[4,24,3584]{2,1,0:T(8,128)(2,1)S(1)}, bf16[4,24,3584]{2,1,0:T(8,128)(2,1)S(1)}, u32[]{:S(2)}, u32[]{:S(2)}) collective-permute-start(bf16[4,24,3584]{2,1,0:T(8,128)(2,1)S(1)} %pad_maximum_fusion.9), channel_id=1, source_target_pairs={{0,3},{1,0},{2,1},{3,2},{4,7},{5,4},{6,5},{7,6},{8,11},{9,8},{10,9... | collective-permute-start | bytes 2064392 | tf_op jit(solution)/shard_map/ppermute | solution.py:39
  203.2 16.7 %collective-permute-start.54 = (bf16[4,24,3584]{2,1,0:T(8,128)(2,1)S(1)}, bf16[4,24,3584]{2,1,0:T(8,128)(2,1)S(1)}, u32[]{:S(2)}, u32[]{:S(2)}) collective-permute-start(bf16[4,24,3584]{2,1,0:T(8,128)(2,1)S(1)} %pad_maximum_fusion.10), channel_id=1, source_target_pairs={{0,1},{1,2},{2,3},{3,0},{4,5},{5,6},{6,7},{7,4},{8,9},{9,10},{10,1... | collective-permute-start | bytes 2064392 | tf_op jit(solution)/shard_map/ppermute | solution.py:40
  205.0 17.8 %collective-permute-start.60 = (bf16[4,24,3712]{2,1,0:T(8,128)(2,1)S(1)}, bf16[4,24,3712]{2,1,0:T(8,128)(2,1)S(1)}, u32[]{:S(2)}, u32[]{:S(2)}) collective-permute-start(bf16[4,24,3712]{2,1,0:T(8,128)(2,1)S(1)} %pad_maximum_fusion.5), channel_id=1, source_target_pairs={{0,12},{4,0},{8,4},{12,8},{1,13},{5,1},{9,5},{13,9},{2,14},{6,2},{... | collective-permute-start | bytes 2138120 | tf_op jit(solution)/shard_map/ppermute | solution.py:39
  206.5 16.5 %collective-permute-start.62 = (bf16[4,24,3712]{2,1,0:T(8,128)(2,1)S(1)}, bf16[4,24,3712]{2,1,0:T(8,128)(2,1)S(1)}, u32[]{:S(2)}, u32[]{:S(2)}) collective-permute-start(bf16[4,24,3712]{2,1,0:T(8,128)(2,1)S(1)} %pad_maximum_fusion.6), channel_id=1, source_target_pairs={{0,4},{4,8},{8,12},{12,0},{1,5},{5,9},{9,13},{13,1},{2,6},{6,10},{... | collective-permute-start | bytes 2138120 | tf_op jit(solution)/shard_map/ppermute | solution.py:40
  238.2 24.4 %collective-permute-start.69 = (bf16[20,3584]{1,0:T(8,128)(2,1)S(1)}, bf16[20,3584]{1,0:T(8,128)(2,1)S(1)}, u32[]{:S(2)}, u32[]{:S(2)}) collective-permute-start(bf16[20,3584]{1,0:T(8,128)(2,1)S(1)} %pad_maximum_fusion.24), channel_id=1, source_target_pairs={{0,224},{16,240},{32,0},{48,16},{64,32},{80,48},{96,64},{112,80},{... | collective-permute-start | bytes 430088 | tf_op jit(solution)/shard_map/ppermute | solution.py:167
  244.7 18.0 %collective-permute-start.70 = (bf16[20,3584]{1,0:T(8,128)(2,1)S(1)}, bf16[20,3584]{1,0:T(8,128)(2,1)S(1)}, u32[]{:S(2)}, u32[]{:S(2)}) collective-permute-start(bf16[20,3584]{1,0:T(8,128)(2,1)S(1)} %pad_maximum_fusion.25), channel_id=1, source_target_pairs={{0,240},{16,224},{32,16},{48,0},{64,48},{80,32},{96,80},{112,64},{... | collective-permute-start | bytes 430088 | tf_op jit(solution)/shard_map/ppermute | solution.py:167
  246.2 16.6 %collective-permute-start.67 = (bf16[20,3584]{1,0:T(8,128)(2,1)S(1)}, bf16[20,3584]{1,0:T(8,128)(2,1)S(1)}, u32[]{:S(2)}, u32[]{:S(2)}) collective-permute-start(bf16[20,3584]{1,0:T(8,128)(2,1)S(1)} %pad_maximum_fusion.23), channel_id=1, source_target_pairs={{0,48},{16,32},{32,80},{48,64},{64,112},{80,96},{96,144},{112,128}... | collective-permute-start | bytes 430088 | tf_op jit(solution)/shard_map/ppermute | solution.py:167
  (61 other events, 568.9 us)
